TPU v7x, 32 devices: a whole 2x2x4 slice. The times are simulated.
32 devices in a mesh: rep: 4 (over x, core), shard: 8 (over z, y).
Axes of the slice: x: 2, y: 2, z: 4, core: 2. Of those that a mesh axis runs over, the one named last changes fastest.
Arguments:
- dense_out: bfloat16 [4096, 128], P(('rep', 'shard')), may hold values from -0.75 to 0.75
- pooled: bfloat16 [4096, 26, 128], P(('rep', 'shard')), may hold values from -0.75 to 0.75
- top_weight: bfloat16 [479, 1024], replicated, may hold values from -0.25 to 0.25
- top_cotangent: bfloat16 [4096, 1024], P(('rep', 'shard')), may hold values from -3 to 3
- indices: int32 [4096, 26, 2], P(('rep', 'shard')), may hold values from 0 to 2047, as said below
Outputs:
- dense_grad: bfloat16 [4096, 128], P(('rep', 'shard'))
- top_grad: float32 [479, 1024], replicated
- bias_grad: float32 [1024], replicated
- table_grad: float32 [26, 2048, 128], P(None, 'shard')
Inputs may be any that keep to these rules, and one draw needn't show every extreme that they name: `indices`: rows r with r // 256 = s are held by shard s. For every device's 128 samples and every table, at most 16 of the device's lookups fall in any one block of 64 rows starting at a multiple of 64, and some such block holds exactly 16.
All inputs are finite; a program needn't handle non-finite values.
Results may differ from a plain program's by a relative error of at most 0.008.
Values may be sent and summed in bfloat16 or wider, within the bound.
A program may use at most 128 MiB of HBM per device.

v0:
```python
import jax
import jax.numpy as jnp
import numpy as np
from jax import lax
from jax.sharding import PartitionSpec as P

R_SHARD = 256
highest = lax.Precision.HIGHEST


def one_hot_sums(rows, keys, height):
    tables_here = rows.shape[0]
    flat_rows = rows.reshape(tables_here, -1, rows.shape[-1])
    flat_keys = keys.reshape(tables_here, -1)

    def per_table(member):
        table_rows, table_keys = member
        levels = lax.broadcasted_iota(jnp.int32, (height, table_keys.shape[0]), 0)
        matches = (levels == table_keys[None, :]).astype(jnp.bfloat16)
        return jnp.dot(matches, table_rows, preferred_element_type=jnp.float32)

    return lax.map(per_table, (flat_rows, flat_keys))


def pair_table(vectors):
    lower_i, lower_j = np.tril_indices(vectors, -1)
    select = np.zeros((vectors * vectors, lower_i.shape[0]), np.float32)
    select[lower_i * vectors + lower_j, np.arange(lower_i.shape[0])] = 1.0
    mirrored = np.zeros((lower_i.shape[0], vectors * vectors), np.float32)
    mirrored[np.arange(lower_i.shape[0]), lower_i * vectors + lower_j] = 1.0
    mirrored[np.arange(lower_i.shape[0]), lower_j * vectors + lower_i] = 1.0
    return (jnp.asarray(select), jnp.asarray(mirrored))


def on_device(dense_out, pooled, top_weight, top_cotangent, indices):
    samples = dense_out.shape[0]
    emb_width = dense_out.shape[1]
    tables = pooled.shape[1]
    lookups = indices.shape[2]
    replicas = lax.axis_size("rep")
    shards = lax.axis_size("shard")
    vectors = tables + 1
    select, mirrored = pair_table(vectors)
    stacked = jnp.concatenate([dense_out[:, None, :], pooled], axis=1)
    gram_matrix = jnp.einsum("bie,bje->bij", stacked, stacked, preferred_element_type=jnp.float32)
    gram_flat = gram_matrix.reshape(samples, vectors * vectors)
    pair_values = jnp.dot(
        gram_flat, select, precision=highest, preferred_element_type=jnp.float32
    ).astype(jnp.bfloat16)
    joined = jnp.concatenate([dense_out, pair_values], axis=1)
    grad_in = lax.dot_general(
        top_cotangent, top_weight, (((1,), (1,)), ((), ())), preferred_element_type=jnp.float32
    )
    top_part = lax.dot_general(
        joined, top_cotangent, (((0,), (0,)), ((), ())), preferred_element_type=jnp.float32
    )
    bias_part = jnp.sum(top_cotangent, axis=0, dtype=jnp.float32)
    pair_grad = grad_in[:, emb_width:]
    mirror = jnp.dot(
        pair_grad, mirrored, precision=highest, preferred_element_type=jnp.float32
    ).reshape(samples, vectors, vectors)
    mirror_high = mirror.astype(jnp.bfloat16)
    mirror_low = (mirror - mirror_high.astype(jnp.float32)).astype(jnp.bfloat16)
    vec_grad = jnp.einsum("bij,bje->bie", mirror_high, stacked, preferred_element_type=jnp.float32)
    vec_grad = vec_grad + jnp.einsum(
        "bij,bje->bie", mirror_low, stacked, preferred_element_type=jnp.float32
    )
    dense_grad = (grad_in[:, :emb_width] + vec_grad[:, 0]).astype(jnp.bfloat16)
    pooled_grad = vec_grad[:, 1:].astype(jnp.bfloat16)
    row_span = R_SHARD // replicas
    blocks = replicas * shards
    per_block = 2 * samples * lookups // blocks
    count_here = samples * lookups
    capacity = blocks * per_block
    by_table = jnp.transpose(indices, (1, 0, 2)).reshape(tables, count_here)
    lookup_rows = jnp.broadcast_to(
        jnp.transpose(pooled_grad, (1, 0, 2))[:, :, None, :], (tables, samples, lookups, emb_width)
    ).reshape(tables, count_here, emb_width)

    def place_table(member):
        table_keys, table_rows = member
        block_row = table_keys // row_span
        later = lax.broadcasted_iota(jnp.int32, (count_here, count_here), 0)
        sooner = lax.broadcasted_iota(jnp.int32, (count_here, count_here), 1)
        earlier = (block_row[None, :] == block_row[:, None]) & (sooner < later)
        slot_row = block_row * per_block + jnp.sum(earlier, axis=1, dtype=jnp.int32)
        levels = lax.broadcasted_iota(jnp.int32, (capacity, count_here), 0)
        placed = levels == slot_row[None, :]
        rows_out = jnp.dot(
            placed.astype(jnp.bfloat16), table_rows, preferred_element_type=jnp.float32
        ).astype(jnp.bfloat16)
        keys_out = (
            jnp.sum(
                jnp.where(placed, (table_keys % R_SHARD + 1)[None, :], 0), axis=1, dtype=jnp.int32
            )
            - 1
        )
        return (rows_out, keys_out)

    send_rows, send_keys = lax.map(place_table, (by_table, lookup_rows))
    top_grad, bias_grad = lax.psum((top_part, bias_part), ("rep", "shard"))
    grouped_rows = send_rows.reshape(tables, shards, replicas * per_block, emb_width)
    grouped_keys = send_keys.reshape(tables, shards, replicas * per_block)
    partial_value = one_hot_sums(
        lax.all_to_all(grouped_rows, "shard", split_axis=1, concat_axis=1, tiled=True),
        lax.all_to_all(grouped_keys, "shard", split_axis=1, concat_axis=1, tiled=True),
        R_SHARD,
    )
    table_grad = lax.psum(partial_value, "rep")
    return (dense_grad, top_grad, bias_grad, table_grad)


def solution(mesh):
    return jax.shard_map(
        on_device,
        mesh=mesh,
        in_specs=(
            P(("rep", "shard"), None),
            P(("rep", "shard"), None, None),
            P(),
            P(("rep", "shard"), None),
            P(("rep", "shard"), None, None),
        ),
        out_specs=(P(("rep", "shard"), None), P(), P(), P(None, "shard", None)),
        check_vma=False,
    )
```

profile of v0, /device:TPU:0, one launch (start us, length us, event | category | flops | bytes accessed | tf_op | source)
XLA Modules:
  0.0 386.4 jit_solution(17738884548787175198)
XLA Ops:
  9.8 2.0 fusion.17
  17.7 2.8 copy.78
  20.6 2.4 copy.77
  24.8 2.9 copy.79
  27.7 2.2 add.78
  34.0 2.4 broadcast_in_dim.67
  36.3 57.8 %while.25 = (s32[]{:T(128)}, bf16[26,512,128]{2,1,0:T(8,128)(2,1)}, s32[26,512]{1,0:T(8,128)S(1)}, s32[26,256]{1,0:T(8,128)S(1)}, bf16[26,256,128]{2,1,0:T(8,128)(2,1)}, /*index=5*/s32[]{:T(128)}, s32[]{:T(128)}) while((s32[]{:T(128)}, bf16[26,512,128]{2,1,0:T(8,128)(2,1)}, s32[26,512]{1,0:T(8,128)S(1)}, s32[26,256]{1,0:T(8,128)S(1)}, ...), condition=%wide.region_6.7_spmd, body=%wide.region_3.6_spmd.sunk | while | flops 34486784 | bytes 224341 | solution.py:100
  95.0 7.3 %all-to-all-start = ((s32[8,1,1664]{2,1,0:T(1,128)}), s32[8,1,1664]{2,1,0:T(1,128)S(1)}, u32[]{:S(2)}, u32[]{:S(2)}) async-start(s32[8,1,1664]{2,1,0:T(1,128)} %reshape.98), calls=%async_computation | async-start | bytes 106496 | tf_op jit(solution)/shard_map/all_to_all | solution.py:106
  102.3 4.8 %copy.87 = bf16[26,8,64,128]{3,2,0,1:T(8,128)(2,1)} copy(bf16[26,8,64,128]{3,2,1,0:T(8,128)(2,1)} %bitcast.71) | data formatting | bytes 6815744 | tf_op jit(solution)/shard_map/reshape | solution.py:102
  107.1 2.0 all-to-all-done
  109.1 4.5 %all-to-all-start.1 = ((bf16[26,8,64,128]{3,2,0,1:T(8,128)(2,1)}), bf16[26,8,64,128]{3,2,0,1:T(8,128)(2,1)}, u32[]{:S(2)}, u32[]{:S(2)}) async-start(bf16[26,8,64,128]{3,2,0,1:T(8,128)(2,1)} %copy.87), calls=%async_computation.1 | async-start | bytes 6815744 | tf_op jit(solution)/shard_map/all_to_all | solution.py:105
  114.5 2.0 fusion.14
  116.5 2.9 reshape.97
  119.4 2.0 convolution_convert_fusion.1
  124.8 73.4 %all-to-all-done.1 = bf16[26,8,64,128]{3,2,0,1:T(8,128)(2,1)} async-done(((bf16[26,8,64,128]{3,2,0,1:T(8,128)(2,1)}), bf16[26,8,64,128]{3,2,0,1:T(8,128)(2,1)}, u32[]{:S(2)}, u32[]{:S(2)}) %all-to-all-start.1) | async-done | bytes 3407904 | tf_op jit(solution)/shard_map/all_to_all | solution.py:105
  198.2 4.8 %copy.88 = bf16[26,8,64,128]{3,2,1,0:T(8,128)(2,1)} copy(bf16[26,8,64,128]{3,2,0,1:T(8,128)(2,1)} %all-to-all-done.1) | data formatting | bytes 6815744 | tf_op jit(solution)/shard_map/all_to_all | solution.py:105
  203.0 47.0 %while.26 = (s32[]{:T(128)}, f32[26,256,128]{2,1,0:T(8,128)}, s32[26,512]{1,0:T(8,128)S(1)}, bf16[26,512,128]{2,1,0:T(8,128)(2,1)}, s32[]{:T(128)}) while((s32[]{:T(128)}, f32[26,256,128]{2,1,0:T(8,128)}, s32[26,512]{1,0:T(8,128)S(1)}, bf16[26,512,128]{2,1,0:T(8,128)(2,1)}, s32[]{:T(128)}) %tuple.72), condition=%wide.region_8.9_spmd, body=%wide.region_7.8_spmd.sunk | while | flops 33685504 | bytes 269377 | solution.py:22
  219.3 1.8 fusion.47
  226.5 1.8 fusion.47
  237.3 1.8 fusion.47
  251.6 38.0 %psum.22 = f32[1024]{0:T(1024)} all-reduce(f32[1024]{0:T(1024)S(1)} %convert_reduce_fusion.1), channel_id=1, replica_groups=mesh['rep'=4,'shard'=8] {'rep','shard'}, use_global_device_ids=true, to_apply=%region_2.3 | all-reduce | flops 1024 | bytes 8192 | tf_op jit(solution)/shard_map/psum | solution.py:101
  289.6 10.4 %all-reduce.3.cloned.1.call-done = f32[479,1024]{1,0:T(8,128)} async-done(((f32[479,1024]{1,0:T(8,128)}), f32[479,1024]{1,0:T(8,128)}) %all-reduce.3.cloned.1.call-update) | async-done | bytes 1962000 | tf_op jit(solution)/shard_map/psum | solution.py:101
  300.1 74.5 %all-reduce.5.cloned.1.call-done = f32[26,256,128]{2,1,0:T(8,128)} async-done(((f32[26,256,128]{2,1,0:T(8,128)}), f32[26,256,128]{2,1,0:T(8,128)}) %all-reduce.5.cloned.1.call-update) | async-done | bytes 3407888 | tf_op jit(solution)/shard_map/psum | solution.py:109
  374.6 3.2 copy.115
  (334 shorter events, 121.2 us)
Async XLA Ops:
  7.2 1.2 copy-start
  7.2 2.6 copy-start.5
  11.8 4.1 %copy-start.7 = (bf16[128,128]{1,0:T(8,128)(2,1)S(1)}, bf16[128,128]{1,0:T(8,128)(2,1)}, u32[]{:S(2)}) copy-start(bf16[128,128]{1,0:T(8,128)(2,1)} %param.11) | copy-start | bytes 98308
  29.9 1.3 copy-start.1
  31.1 2.6 copy-start.8
  95.0 14.1 %all-to-all-start = ((s32[8,1,1664]{2,1,0:T(1,128)}), s32[8,1,1664]{2,1,0:T(1,128)S(1)}, u32[]{:S(2)}, u32[]{:S(2)}) async-start(s32[8,1,1664]{2,1,0:T(1,128)} %reshape.98), calls=%async_computation | async-start | bytes 106496 | tf_op jit(solution)/shard_map/all_to_all | solution.py:106
  109.1 89.1 %all-to-all-start.1 = ((bf16[26,8,64,128]{3,2,0,1:T(8,128)(2,1)}), bf16[26,8,64,128]{3,2,0,1:T(8,128)(2,1)}, u32[]{:S(2)}, u32[]{:S(2)}) async-start(bf16[26,8,64,128]{3,2,0,1:T(8,128)(2,1)} %copy.87), calls=%async_computation.1 | async-start | bytes 6815744 | tf_op jit(solution)/shard_map/all_to_all | solution.py:105
  113.6 186.5 %all-reduce.3.cloned.1.call-start = ((), (), s32[]{:S(2)}) async-start(), calls=%async_computation.2 | async-start | bytes 3932160 | tf_op jit(solution)/shard_map/psum | solution.py:101
  114.5 4.9 %copy-start.4 = (f32[729,351]{1,0:T(8,128)S(1)}, f32[729,351]{1,0:T(8,128)}, u32[]{:S(2)}) copy-start(f32[729,351]{1,0:T(8,128)} %constant.104.clone) | copy-start | bytes 3070552
  116.5 4.9 %copy-start.3 = (bf16[128,1024]{1,0:T(8,128)(2,1)S(1)}, bf16[128,1024]{1,0:T(8,128)(2,1)}, u32[]{:S(2)}) copy-start(bf16[128,1024]{1,0:T(8,128)(2,1)} %param.14) | copy-start | bytes 786436
  116.5 4.9 %copy-start.6 = (bf16[128,128]{0,1:T(8,128)(2,1)S(1)}, bf16[128,128]{0,1:T(8,128)(2,1)}, u32[]{:S(2)}) copy-start(bf16[128,128]{0,1:T(8,128)(2,1)} %copy.81) | copy-start | bytes 98308
  123.2 251.4 %all-reduce.5.cloned.1.call-start = ((), (), s32[]{:S(2)}) async-start(), calls=%async_computation.3 | async-start | bytes 6815744 | tf_op jit(solution)/shard_map/psum | solution.py:109
  374.6 3.2 copy-start.2
Sparse Core Ops, SparseCore 0:
  123.3 176.7 all-reduce.2
  303.0 71.5 all-reduce.4
where the time goes:
time: 389 us; the launch traced here: 386 us
  waiting for transfers between devices  160 us (41%)
  matrix products  105 us (27%)
  local copies, waits for them, and re-layouts  41.3 us (11%)
  blocking collectives  38 us (10%)
  other arithmetic  14.6 us (4%)
  between operations  14.3 us (4%)
  starting transfers between devices  12 us (3%)
    psum x1, waiting for transfers between devices, on_device(): table_grad = lax.psum(partial_value, 'rep')  74.5 us
    all_to_all x1, waiting for transfers between devices, on_device(): lax.all_to_all(grouped_rows, 'shard', split_axis=1, concat_axis=1, tiled=...  73.4 us
    dot_general x26, matrix products, per_table(): return jnp.dot(matches, table_rows, preferred_element_type=jnp.float32)  46.8 us
    dot_general x26, matrix products, place_table(): jnp.dot(placed.astype(jnp.bfloat16), table_rows, preferred_element_type=j...  45.3 us
    psum x1, blocking collectives, on_device(): top_grad, bias_grad = lax.psum((top_part, bias_part), ('rep', 'shard'))  38 us
    unnamed x25, local copies, waits for them, and re-layouts  11.4 us
    psum x1, waiting for transfers between devices, on_device(): top_grad, bias_grad = lax.psum((top_part, bias_part), ('rep', 'shard'))  10.4 us
  transfers between devices with their start and end apart: 4, of which 4 were waited for; matrix products, arithmetic and copies ran while one was open for 18% of the time, Pallas kernels for 0%

commit v1 on v0

--- a/solution.py
+++ b/solution.py
@@ -106,7 +106,11 @@
         lax.all_to_all(grouped_keys, "shard", split_axis=1, concat_axis=1, tiled=True),
         R_SHARD,
     )
-    table_grad = lax.psum(partial_value, "rep")
+    table_grad = partial_value
+    for hop in (1, 2):
+        table_grad = table_grad + lax.ppermute(
+            table_grad, "rep", [(dev, dev ^ hop) for dev in range(4)]
+        )
     return (dense_grad, top_grad, bias_grad, table_grad)
 
 

time: 389 us -> 407 us (1.046)
  blocking collectives: 38 us -> 103 us
  waiting for transfers between devices: 160 us -> 105 us
  other arithmetic: 14.6 us -> 24 us
    psum x1 -> x0, waiting for transfers between devices: 74.5 us -> none  [on_device(): table_grad = lax.psum(partial_value, 'rep')]
    psum x1, blocking collectives: 38 us -> 103 us  [on_device(): top_grad, bias_grad = lax.psum((top_part, bias_part), ('rep', 'shard'))]
    psum x1, waiting for transfers between devices: 10.4 us -> 23.2 us  [on_device(): top_grad, bias_grad = lax.psum((top_part, bias_part), ('rep', 'shard'))]
    add x0 -> x2, other arithmetic: none -> 9.44 us  [on_device(): table_grad + lax.ppermute(table_grad, 'rep', [(dev, dev ^ hop) for dev in...]
    ppermute x0 -> x2, waiting for transfers between devices: none -> 6.24 us  [on_device(): lax.ppermute(table_grad, 'rep', [(dev, dev ^ hop) for dev in range(4)])]
    unnamed x25 -> x20, local copies, waits for them, and re-layouts: 11.4 us -> 8.86 us
  transfers between devices with their start and end apart: 4 -> 5, of which waited for: 4 -> 4; matrix products, arithmetic and copies ran while one was open for 18% -> 5% of each run, Pallas kernels for 0% -> 0%
where the time goes in v1:
time: 407 us; the launch traced here: 404 us
  matrix products  105 us (26%)
  waiting for transfers between devices  105 us (26%)
  blocking collectives  103 us (25%)
  local copies, waits for them, and re-layouts  38.8 us (10%)
  other arithmetic  24 us (6%)
  between operations  14.3 us (4%)
  starting transfers between devices  13.5 us (3%)
    psum x1, blocking collectives, on_device(): top_grad, bias_grad = lax.psum((top_part, bias_part), ('rep', 'shard'))  103 us
    all_to_all x1, waiting for transfers between devices, on_device(): lax.all_to_all(grouped_rows, 'shard', split_axis=1, concat_axis=1, tiled=...  73.6 us
    dot_general x26, matrix products, per_table(): return jnp.dot(matches, table_rows, preferred_element_type=jnp.float32)  46.8 us
    dot_general x26, matrix products, place_table(): jnp.dot(placed.astype(jnp.bfloat16), table_rows, preferred_element_type=j...  45.3 us
    psum x1, waiting for transfers between devices, on_device(): top_grad, bias_grad = lax.psum((top_part, bias_part), ('rep', 'shard'))  23.2 us
    add x2, other arithmetic, on_device(): table_grad + lax.ppermute(table_grad, 'rep', [(dev, dev ^ hop) for dev in...  9.44 us
    unnamed x20, local copies, waits for them, and re-layouts  8.86 us
  transfers between devices with their start and end apart: 5, of which 4 were waited for; matrix products, arithmetic and copies ran while one was open for 5% of the time, Pallas kernels for 0%

profile of v1, /device:TPU:0, one launch (start us, length us, event | category | flops | bytes accessed | tf_op | source)
XLA Modules:
  0.0 404.2 jit_solution(3883946638529452408)
XLA Ops:
  9.8 2.0 fusion.17
  17.7 2.8 copy.78
  20.6 2.4 copy.77
  24.8 2.9 copy.79
  27.7 2.2 add.82
  33.9 2.4 broadcast_in_dim.67
  36.3 57.8 %while.25 = (s32[]{:T(128)}, bf16[26,512,128]{2,1,0:T(8,128)(2,1)}, s32[26,512]{1,0:T(8,128)S(1)}, s32[26,256]{1,0:T(8,128)S(1)}, bf16[26,256,128]{2,1,0:T(8,128)(2,1)}, /*index=5*/s32[]{:T(128)}, s32[]{:T(128)}) while((s32[]{:T(128)}, bf16[26,512,128]{2,1,0:T(8,128)(2,1)}, s32[26,512]{1,0:T(8,128)S(1)}, s32[26,256]{1,0:T(8,128)S(1)}, ...), condition=%wide.region_6.7_spmd, body=%wide.region_3.6_spmd.sunk | while | flops 34486784 | bytes 224341 | solution.py:100
  95.0 7.3 %all-to-all-start = ((s32[8,1,1664]{2,1,0:T(1,128)}), s32[8,1,1664]{2,1,0:T(1,128)S(1)}, u32[]{:S(2)}, u32[]{:S(2)}) async-start(s32[8,1,1664]{2,1,0:T(1,128)} %reshape.98), calls=%async_computation | async-start | bytes 106496 | tf_op jit(solution)/shard_map/all_to_all | solution.py:106
  102.3 4.8 %copy.87 = bf16[26,8,64,128]{3,2,0,1:T(8,128)(2,1)} copy(bf16[26,8,64,128]{3,2,1,0:T(8,128)(2,1)} %bitcast.71) | data formatting | bytes 6815744 | tf_op jit(solution)/shard_map/reshape | solution.py:102
  107.1 2.0 all-to-all-done
  109.1 4.5 %all-to-all-start.1 = ((bf16[26,8,64,128]{3,2,0,1:T(8,128)(2,1)}), bf16[26,8,64,128]{3,2,0,1:T(8,128)(2,1)}, u32[]{:S(2)}, u32[]{:S(2)}) async-start(bf16[26,8,64,128]{3,2,0,1:T(8,128)(2,1)} %copy.87), calls=%async_computation.1 | async-start | bytes 6815744 | tf_op jit(solution)/shard_map/all_to_all | solution.py:105
  115.3 73.6 %all-to-all-done.1 = bf16[26,8,64,128]{3,2,0,1:T(8,128)(2,1)} async-done(((bf16[26,8,64,128]{3,2,0,1:T(8,128)(2,1)}), bf16[26,8,64,128]{3,2,0,1:T(8,128)(2,1)}, u32[]{:S(2)}, u32[]{:S(2)}) %all-to-all-start.1) | async-done | bytes 3407904 | tf_op jit(solution)/shard_map/all_to_all | solution.py:105
  188.9 4.8 %copy.88 = bf16[26,8,64,128]{3,2,1,0:T(8,128)(2,1)} copy(bf16[26,8,64,128]{3,2,0,1:T(8,128)(2,1)} %all-to-all-done.1) | data formatting | bytes 6815744 | tf_op jit(solution)/shard_map/all_to_all | solution.py:105
  193.7 47.0 %while.26 = (s32[]{:T(128)}, f32[26,256,128]{2,1,0:T(8,128)}, s32[26,512]{1,0:T(8,128)S(1)}, bf16[26,512,128]{2,1,0:T(8,128)(2,1)}, s32[]{:T(128)}) while((s32[]{:T(128)}, f32[26,256,128]{2,1,0:T(8,128)}, s32[26,512]{1,0:T(8,128)S(1)}, bf16[26,512,128]{2,1,0:T(8,128)(2,1)}, s32[]{:T(128)}) %tuple.70), condition=%wide.region_8.9_spmd, body=%wide.region_7.8_spmd.sunk | while | flops 33685504 | bytes 269377 | solution.py:22
  195.6 1.8 fusion.47
  240.7 6.2 %collective-permute-done = f32[26,256,128]{2,1,0:T(8,128)S(1)} collective-permute-done((f32[26,256,128]{2,1,0:T(8,128)}, f32[26,256,128]{2,1,0:T(8,128)S(1)}, u32[]{:S(2)}, u32[]{:S(2)}) %collective-permute-start) | collective-permute-done | bytes 3407904 | tf_op jit(solution)/shard_map/ppermute | solution.py:111
  247.0 4.2 %add.84 = f32[26,256,128]{2,1,0:T(8,128)} add(f32[26,256,128]{2,1,0:T(8,128)} %get-tuple-element.119, f32[26,256,128]{2,1,0:T(8,128)S(1)} %collective-permute-done) | non-fusion elementwise | flops 851968 | bytes 10223616 | tf_op jit(solution)/shard_map/add | solution.py:111
  252.7 2.0 fusion.14
  254.8 2.9 reshape.97
  257.7 2.0 convolution_convert_fusion.1
  263.0 102.8 %psum.15 = f32[1024]{0:T(1024)} all-reduce(f32[1024]{0:T(1024)S(1)} %convert_reduce_fusion.1), channel_id=1, replica_groups=mesh['rep'=4,'shard'=8] {'rep','shard'}, use_global_device_ids=true, to_apply=%region_2.3 | all-reduce | flops 1024 | bytes 8192 | tf_op jit(solution)/shard_map/psum | solution.py:101
  365.8 5.3 %add.85 = f32[26,256,128]{2,1,0:T(8,128)} add(f32[26,256,128]{2,1,0:T(8,128)} %add.84, f32[26,256,128]{2,1,0:T(8,128)} %collective-permute-done.1) | non-fusion elementwise | flops 851968 | bytes 10223616 | tf_op jit(solution)/shard_map/add | solution.py:111
  371.1 23.2 %all-reduce.2.cloned.1.call-done = f32[479,1024]{1,0:T(8,128)} async-done(((f32[479,1024]{1,0:T(8,128)}), f32[479,1024]{1,0:T(8,128)}) %all-reduce.2.cloned.1.call-update) | async-done | bytes 1962000 | tf_op jit(solution)/shard_map/psum | solution.py:101
  394.3 3.0 copy.114
  (332 shorter events, 123.8 us)
Async XLA Ops:
  7.2 1.2 copy-start
  7.2 2.6 copy-start.4
  11.8 4.1 %copy-start.5 = (bf16[128,128]{1,0:T(8,128)(2,1)S(1)}, bf16[128,128]{1,0:T(8,128)(2,1)}, u32[]{:S(2)}) copy-start(bf16[128,128]{1,0:T(8,128)(2,1)} %param.11) | copy-start | bytes 98308
  29.9 1.2 copy-start.1
  31.1 2.6 copy-start.6
  95.0 14.1 %all-to-all-start = ((s32[8,1,1664]{2,1,0:T(1,128)}), s32[8,1,1664]{2,1,0:T(1,128)S(1)}, u32[]{:S(2)}, u32[]{:S(2)}) async-start(s32[8,1,1664]{2,1,0:T(1,128)} %reshape.98), calls=%async_computation | async-start | bytes 106496 | tf_op jit(solution)/shard_map/all_to_all | solution.py:106
  109.1 79.8 %all-to-all-start.1 = ((bf16[26,8,64,128]{3,2,0,1:T(8,128)(2,1)}), bf16[26,8,64,128]{3,2,0,1:T(8,128)(2,1)}, u32[]{:S(2)}, u32[]{:S(2)}) async-start(bf16[26,8,64,128]{3,2,0,1:T(8,128)(2,1)} %copy.87), calls=%async_computation.1 | async-start | bytes 6815744 | tf_op jit(solution)/shard_map/all_to_all | solution.py:105
  113.6 280.7 %all-reduce.2.cloned.1.call-start = ((), (), s32[]{:S(2)}) async-start(), calls=%async_computation.2 | async-start | bytes 3932160 | tf_op jit(solution)/shard_map/psum | solution.py:101
  240.7 6.2 %collective-permute-start = (f32[26,256,128]{2,1,0:T(8,128)}, f32[26,256,128]{2,1,0:T(8,128)S(1)}, u32[]{:S(2)}, u32[]{:S(2)}) collective-permute-start(f32[26,256,128]{2,1,0:T(8,128)} %get-tuple-element.119), channel_id=1, source_target_pairs={{0,8},{8,0},{16,24},{24,16},{1,9},{9,1},{17,25},{25,17},{2,10},{10... | collective-permute-start | bytes 10223624 | tf_op jit(solution)/shard_map/ppermute | solution.py:111
  251.1 114.7 %collective-permute-start.1 = (f32[26,256,128]{2,1,0:T(8,128)}, f32[26,256,128]{2,1,0:T(8,128)}, u32[]{:S(2)}, u32[]{:S(2)}) collective-permute-start(f32[26,256,128]{2,1,0:T(8,128)} %add.84), channel_id=1, source_target_pairs={{0,16},{8,24},{16,0},{24,8},{1,17},{9,25},{17,1},{25,9},{2,18},{10... | collective-permute-start | bytes 10223624 | tf_op jit(solution)/shard_map/ppermute | solution.py:111
  252.7 4.9 %copy-start.3 = (f32[729,351]{1,0:T(8,128)S(1)}, f32[729,351]{1,0:T(8,128)}, u32[]{:S(2)}) copy-start(f32[729,351]{1,0:T(8,128)} %constant.104.clone) | copy-start | bytes 3070552
  254.8 4.9 %copy-start.2 = (bf16[128,1024]{1,0:T(8,128)(2,1)S(1)}, bf16[128,1024]{1,0:T(8,128)(2,1)}, u32[]{:S(2)}) copy-start(bf16[128,1024]{1,0:T(8,128)(2,1)} %param.14) | copy-start | bytes 786436
Sparse Core Ops, SparseCore 0:
  261.5 132.7 all-reduce.1
